TPU v7x, 32 devices: a whole 2x2x4 slice. The times are simulated.
32 devices in a mesh: row: 4 (over y, core), col: 8 (over z, x).
Axes of the slice: x: 2, y: 2, z: 4, core: 2. Of those that a mesh axis runs over, the one named last changes fastest.
Arguments:
- vectors: bfloat16 [4, 8, 128, 384], P('row', 'col'), may hold values from -6 to 6
- near_blocks: bfloat16 [4, 8, 9, 384, 384], P('row', 'col'), may hold values from -0.15625 to 0.15625
- near_source: int32 [4, 8, 9], P('row', 'col'), may hold values from 0 to 8, each once within a row
- near_count: int32 [4, 8], P('row', 'col'), may hold values from 1 to 9
- basis_col: bfloat16 [4, 8, 64, 384], P('row', 'col'), may hold values from -0.3125 to 0.3125
- transfer_col: bfloat16 [4, 8, 64, 64], P('row', 'col'), may hold values from -0.25 to 0.25
- leaf_couple: bfloat16 [4, 8, 3, 5, 64, 64], P('row', 'col'), may hold values from -0.1875 to 0.1875
- coupling: bfloat16 [4, 4, 64, 64], P('row'), may hold values from -0.75 to 0.75
- distant_region_list: int32 [4, 4], P('row'), may hold values from 0 to 3, each once within a row
- transfer_row: bfloat16 [4, 8, 64, 64], P('row', 'col'), may hold values from -0.75 to 0.75
- basis_row: bfloat16 [4, 8, 64, 384], P('row', 'col'), may hold values from -0.75 to 0.75
Outputs:
- product: bfloat16 [4, 8, 128, 384], P('row', 'col')
Inputs may be any that keep to these rules, and one draw needn't show every extreme that they name: `near_source`: the 9 slots of a leaf name the nine neighbourhood cells once each. Only the first near_count slots of a leaf are live. `distant_region_list`: each region's list names every region once.
All inputs are finite; a program needn't handle non-finite values.
Results may differ from a plain program's by a relative error of at most 0.013.
Values may be sent and summed in bfloat16 or wider, within the bound.
A program may use at most 64 MiB of HBM per device.

v0:
```python
import jax
import jax.numpy as jnp
from jax import lax
from jax.sharding import PartitionSpec as P


def from_behind(value, axis, steps):
    count = lax.axis_size(axis)
    pairs = [(source, (source + steps) % count) for source in range(count)]
    return lax.ppermute(value, axis, pairs)


def padded_2(cells, sides, width):
    for axis, dim in sides:
        count = lax.axis_size(axis)
        head = lax.slice_in_dim(cells, 0, width, axis=dim)
        tail = lax.slice_in_dim(cells, cells.shape[dim] - width, cells.shape[dim], axis=dim)
        cells = jnp.concatenate(
            [
                lax.ppermute(tail, axis, [(i, (i + 1) % count) for i in range(count)]),
                cells,
                lax.ppermute(head, axis, [((i + 1) % count, i) for i in range(count)]),
            ],
            axis=dim,
        )
    return cells


def per_device(
    vectors,
    near_blocks,
    near_source,
    near_count,
    basis_col,
    transfer_col,
    leaf_couple,
    coupling,
    distant_region_list,
    transfer_row,
    basis_row,
):
    upper_limit = lax.Precision.HIGHEST
    leading = from_behind(vectors, "row", -1)
    leading = from_behind(leading, "col", -1)
    padded = padded_2(leading, (("row", 0), ("col", 1)), 1)
    table = padded.reshape(9, padded.shape[2], padded.shape[3])
    picked = jnp.take(table, near_source[0, 0], axis=0)
    slots = jnp.arange(picked.shape[0], dtype=jnp.int32)
    live_mask = (slots < near_count[0, 0])[:, None, None]
    picked = jnp.where(live_mask, picked, jnp.zeros_like(picked))
    near_part = jnp.einsum(
        "svp,spq->vq", picked, near_blocks[0, 0], preferred_element_type=jnp.float32
    )
    incoming_leaf = lax.dot_general(
        vectors[0, 0], basis_col[0, 0], (((1,), (1,)), ((), ())), preferred_element_type=jnp.float32
    )
    next_row = from_behind(incoming_leaf.astype(jnp.bfloat16), "row", -1).astype(
        incoming_leaf.dtype
    )
    second_row = from_behind(incoming_leaf.astype(jnp.bfloat16), "row", -2).astype(
        incoming_leaf.dtype
    )
    three_rows = jnp.stack([incoming_leaf, next_row, second_row], axis=0)
    leaves_of_rows = lax.all_gather(
        three_rows[:, None].astype(jnp.bfloat16), "col", axis=1, tiled=True
    ).astype(jnp.float32)
    col_count = lax.axis_size("col")
    rolled = jnp.roll(leaves_of_rows, -(lax.axis_index("col") + 3), axis=1)[:, : col_count - 3]
    band = jnp.einsum(
        "dfvk,dfkl->vl", rolled, leaf_couple[0, 0].astype(jnp.float32), precision=upper_limit
    )
    upward = jnp.dot(incoming_leaf, transfer_col[0, 0].astype(jnp.float32), precision=upper_limit)
    row_count = lax.axis_size("row")
    own_region = lax.psum(upward.astype(jnp.bfloat16), "col").astype(jnp.float32)
    regions = lax.all_gather(
        own_region[None].astype(jnp.bfloat16), "row", axis=0, tiled=True
    ).astype(jnp.float32)
    listing = distant_region_list[0]
    far_mask = ((listing - lax.axis_index("row")) % row_count >= 3).astype(jnp.float32)
    far_coeff = jnp.take(regions, listing, axis=0) * far_mask[:, None, None]
    outgoing_region = jnp.einsum(
        "fvk,fkl->vl", far_coeff, coupling[0].astype(jnp.float32), precision=upper_limit
    )
    leaf_out = band + jnp.dot(
        outgoing_region, transfer_row[0, 0].astype(jnp.float32), precision=upper_limit
    )
    far_part = jnp.dot(leaf_out, basis_row[0, 0].astype(jnp.float32), precision=upper_limit)
    return (near_part + far_part).astype(jnp.bfloat16)[None, None]


def solution(mesh):
    placed = (
        P("row", "col", None, None),
        P("row", "col", None, None, None),
        P("row", "col", None),
        P("row", "col"),
        P("row", "col", None, None),
        P("row", "col", None, None),
        P("row", "col", None, None, None, None),
        P("row", None, None, None),
        P("row", None),
        P("row", "col", None, None),
        P("row", "col", None, None),
    )
    return jax.shard_map(
        per_device,
        mesh=mesh,
        in_specs=placed,
        out_specs=P("row", "col", None, None),
        check_vma=False,
    )
```

profile of v0, /device:TPU:1, one launch (start us, length us, event | category | flops | bytes accessed | tf_op | source)
XLA Modules:
  0.0 112.0 jit_solution(17042163950172736035)
XLA Ops:
  0.0 0.0 copy-start
  0.0 0.0 copy-start.3
  0.0 0.0 collective-permute-start
  0.0 1.2 %fusion.37 = (bf16[128,64]{0,1:T(8,128)(2,1)S(1)}, f32[128,64]{0,1:T(8,128)S(1)}) fusion(bf16[1,1,64,384]{3,2,1,0:T(8,128)(2,1)} %param.15, bf16[1,1,128,384]{3,2,1,0:T(8,128)(2,1)} %param.11), kind=kOutput, calls=%fused_computation.62 | convolution fusion | flops 6299648 | bytes 196608 | tf_op jit(solution)/shard_map/dot_general | solution.py:54
  1.2 2.7 %collective-permute-start.7 = (bf16[128,64]{0,1:T(8,128)(2,1)S(1)}, bf16[128,64]{0,1:T(8,128)(2,1)S(1)}, u32[]{:S(2)}, u32[]{:S(2)}) collective-permute-start(bf16[128,64]{0,1:T(8,128)(2,1)S(1)} %get-tuple-element.7), channel_id=1, source_target_pairs={{0,16},{8,24},{16,0},{24,8},{1,17},{9,25},{17,1},{25,9},{2,18},{10... | collective-permute-start | bytes 49160 | tf_op jit(solution)/shard_map/ppermute | solution.py:10
  4.0 0.3 collective-permute-start.6
  4.3 0.7 fusion.30
  5.6 0.7 compare_and_fusion.1
  6.3 0.9 fusion.7
  7.2 30.1 %psum.7 = bf16[1,128,64]{1,2,0:T(8,128)(2,1)S(1)} all-reduce(bf16[1,128,64]{1,2,0:T(8,128)(2,1)S(1)} %fusion.7), channel_id=1, replica_groups=mesh['row'=4,'col'=8] {'col'}, use_global_device_ids=true, to_apply=%region_0.1 | all-reduce | flops 8192 | bytes 32768 | tf_op jit(solution)/shard_map/psum | solution.py:74
  37.4 12.6 %all_gather.7 = bf16[4,128,64]{1,2,0:T(8,128)(2,1)S(1)} all-gather(bf16[1,128,64]{1,2,0:T(8,128)(2,1)S(1)} %psum.7), channel_id=1, replica_groups=mesh['row'=4,'col'=8] {'row'}, dimensions={0}, use_global_device_ids=true | all-gather | bytes 81920 | tf_op jit(solution)/shard_map/all_gather | solution.py:75
  50.0 0.7 fusion.31
  50.6 0.7 compare_and_fusion
  51.3 0.6 gather_fusion.1
  51.9 1.2 %convolution_bitcast_fusion = f32[128,64]{1,0:T(8,128)S(1)} fusion(f32[4,128,64]{1,2,0:T(8,128)S(1)} %gather_fusion.1, bf16[1,4,64,64]{3,2,1,0:T(8,128)(2,1)} %param.18, f32[4]{0:T(128)S(1)} %get-tuple-element.6, pred[4]{0:T(512)(128)(4,1)S(1)} %get-tuple-element.5), kind=kOutput, calls=%fused_computation.9 | convolution fusion | flops 25231360 | bytes 196628 | tf_op jit(solution)/shard_map/fvk,fkl->vl/dot_general | solution.py:81
  53.1 0.0 collective-permute-done
  53.1 0.1 collective-permute-start.1
  53.2 0.0 collective-permute-done.7
  53.2 0.0 collective-permute-done.6
  53.2 4.1 %collective-permute-done.1 = bf16[1,1,128,384]{3,2,1,0:T(8,128)(2,1)S(1)} collective-permute-done((bf16[1,1,128,384]{3,2,1,0:T(8,128)(2,1)S(1)}, bf16[1,1,128,384]{3,2,1,0:T(8,128)(2,1)S(1)}, u32[]{:S(2)}, u32[]{:S(2)}) %collective-permute-start.1) | collective-permute-done | bytes 98336 | tf_op jit(solution)/shard_map/ppermute | solution.py:10
  57.4 2.1 %collective-permute-start.2 = (bf16[1,1,128,384]{3,2,1,0:T(8,128)(2,1)S(1)}, bf16[1,1,128,384]{3,2,1,0:T(8,128)(2,1)S(1)}, u32[]{:S(2)}, u32[]{:S(2)}) collective-permute-start(bf16[1,1,128,384]{3,2,1,0:T(8,128)(2,1)S(1)} %collective-permute-done.1), channel_id=1, source_target_pairs={{0,8},{8,16},{16,24},{24,0},{1,9},{9,17},{17,25},{25,1},{2,10},{10... | collective-permute-start | bytes 294920 | tf_op jit(solution)/shard_map/ppermute | solution.py:20
  59.5 25.3 %all_gather.6 = bf16[3,8,128,64]{2,3,1,0:T(8,128)(2,1)S(1)} all-gather(bf16[3,1,128,64]{2,3,1,0:T(8,128)(2,1)S(1)} %pad_maximum_fusion.1), channel_id=1, replica_groups=mesh['row'=4,'col'=8] {'col'}, dimensions={1}, use_global_device_ids=true | all-gather | bytes 442368 | tf_op jit(solution)/shard_map/all_gather | solution.py:64
  84.8 4.8 %collective-permute-start.3 = (bf16[1,1,128,384]{3,2,1,0:T(8,128)(2,1)S(1)}, bf16[1,1,128,384]{3,2,1,0:T(8,128)(2,1)S(1)}, u32[]{:S(2)}, u32[]{:S(2)}) collective-permute-start(bf16[1,1,128,384]{3,2,1,0:T(8,128)(2,1)S(1)} %collective-permute-done.1), channel_id=1, source_target_pairs={{8,0},{16,8},{24,16},{0,24},{9,1},{17,9},{25,17},{1,25},{10,2},{18... | collective-permute-start | bytes 294920 | tf_op jit(solution)/shard_map/ppermute | solution.py:22
  89.6 0.0 collective-permute-done.2
  89.6 3.4 %collective-permute-done.3 = bf16[1,1,128,384]{3,2,1,0:T(8,128)(2,1)S(1)} collective-permute-done((bf16[1,1,128,384]{3,2,1,0:T(8,128)(2,1)S(1)}, bf16[1,1,128,384]{3,2,1,0:T(8,128)(2,1)S(1)}, u32[]{:S(2)}, u32[]{:S(2)}) %collective-permute-start.3) | collective-permute-done | bytes 98336 | tf_op jit(solution)/shard_map/ppermute | solution.py:22
  93.0 2.5 %collective-permute-start.5 = (bf16[3,1,128,384]{3,2,1,0:T(8,128)(2,1)S(1)}, bf16[3,1,128,384]{3,2,1,0:T(8,128)(2,1)S(1)}, u32[]{:S(2)}, u32[]{:S(2)}) collective-permute-start(bf16[3,1,128,384]{3,2,1,0:T(8,128)(2,1)S(1)} %constant_dynamic-update-slice_fusion), channel_id=1, source_target_pairs={{1,0},{2,1},{3,2},{4,3},{5,4},{6,5},{7,6},{0,7},{9,8},{10,9},{11,1... | collective-permute-start | bytes 884744 | tf_op jit(solution)/shard_map/ppermute | solution.py:22
  95.5 0.0 collective-permute-start.4
  95.5 1.2 %convolution_bitcast_fusion.1 = f32[128,64]{1,0:T(8,128)S(1)} fusion(s32[]{:T(128)S(6)} %select_n.72, bf16[3,8,128,64]{2,3,1,0:T(8,128)(2,1)S(1)} %all_gather.6, bf16[1,1,3,5,64,64]{5,4,3,2,1,0:T(8,128)(2,1)} %param.17), kind=kOutput, calls=%fused_computation.10 | convolution fusion | flops 16515072 | bytes 548868 | tf_op jit(solution)/shard_map/dfvk,dfkl->vl/dot_general | solution.py:69
  96.7 0.0 copy-done.3
  96.8 0.8 convolution_add_fusion.1
  97.5 9.9 %collective-permute-done.5 = bf16[3,1,128,384]{3,2,1,0:T(8,128)(2,1)S(1)} collective-permute-done((bf16[3,1,128,384]{3,2,1,0:T(8,128)(2,1)S(1)}, bf16[3,1,128,384]{3,2,1,0:T(8,128)(2,1)S(1)}, u32[]{:S(2)}, u32[]{:S(2)}) %collective-permute-start.5) | collective-permute-done | bytes 294944 | tf_op jit(solution)/shard_map/ppermute | solution.py:22
  107.4 0.0 collective-permute-done.4
  107.4 0.1 pad_maximum_fusion
  107.5 1.7 %gather_fusion = bf16[9,128,384]{2,1,0:T(8,128)(2,1)} fusion(bf16[9,128,384]{2,1,0:T(8,128)(2,1)S(1)} %bitcast.66, s32[1024]{0:T(1024)S(1)} %pad_clamp_fusion.1), kind=kCustom, calls=%fused_computation | custom fusion | bytes 1769508 | tf_op jit(solution)/shard_map/jit(_take)/gather | solution.py:47
  109.2 0.0 copy-start.1
  109.2 0.0 copy-start.2
  109.2 0.0 copy-done
  109.2 1.9 %fusion.2 = f32[128,384]{1,0:T(8,128)S(1)} fusion(bf16[1,1,9,384,384]{4,3,2,1,0:T(8,128)(2,1)S(1)} %copy-done, bf16[9,128,384]{2,1,0:T(8,128)(2,1)} %gather_fusion, pred[9]{0:T(512)(128)(4,1)S(1)} %get-tuple-element.9, pred[9]{0:T(512)(128)(4,1)S(1)} %get-tuple-element.10), kind=kOutput, calls=%fused_computation.5 | convolution fusion | flops 340623360 | bytes 3735570 | tf_op jit(solution)/shard_map/svp,spq->vq/dot_general | solution.py:51
  111.1 0.0 copy-done.1
  111.1 0.0 copy-done.2
  111.1 0.9 fusion.6
  (7 shorter events, 0.1 us)
Async XLA Ops:
  0.0 109.2 %copy-start = (bf16[1,1,9,384,384]{4,3,2,1,0:T(8,128)(2,1)S(1)}, bf16[1,1,9,384,384]{4,3,2,1,0:T(8,128)(2,1)}, u32[]{:S(2)}) copy-start(bf16[1,1,9,384,384]{4,3,2,1,0:T(8,128)(2,1)} %param.12) | copy-start | bytes 7962628
  0.0 96.7 %copy-start.3 = (bf16[1,1,64,64]{3,2,1,0:T(8,128)(2,1)S(1)}, bf16[1,1,64,64]{3,2,1,0:T(8,128)(2,1)}, u32[]{:S(2)}) copy-start(bf16[1,1,64,64]{3,2,1,0:T(8,128)(2,1)} %param.20) | copy-start | bytes 24580
  0.0 53.1 %collective-permute-start = (bf16[1,1,128,384]{3,2,1,0:T(8,128)(2,1)}, bf16[1,1,128,384]{3,2,1,0:T(8,128)(2,1)S(1)}, u32[]{:S(2)}, u32[]{:S(2)}) collective-permute-start(bf16[1,1,128,384]{3,2,1,0:T(8,128)(2,1)} %param.11), channel_id=1, source_target_pairs={{0,24},{8,0},{16,8},{24,16},{1,25},{9,1},{17,9},{25,17},{2,26},{10... | collective-permute-start | bytes 294920 | tf_op jit(solution)/shard_map/ppermute | solution.py:10
  1.2 52.0 %collective-permute-start.7 = (bf16[128,64]{0,1:T(8,128)(2,1)S(1)}, bf16[128,64]{0,1:T(8,128)(2,1)S(1)}, u32[]{:S(2)}, u32[]{:S(2)}) collective-permute-start(bf16[128,64]{0,1:T(8,128)(2,1)S(1)} %get-tuple-element.7), channel_id=1, source_target_pairs={{0,16},{8,24},{16,0},{24,8},{1,17},{9,25},{17,1},{25,9},{2,18},{10... | collective-permute-start | bytes 49160 | tf_op jit(solution)/shard_map/ppermute | solution.py:10
  4.0 49.2 %collective-permute-start.6 = (bf16[128,64]{0,1:T(8,128)(2,1)S(1)}, bf16[128,64]{0,1:T(8,128)(2,1)S(1)}, u32[]{:S(2)}, u32[]{:S(2)}) collective-permute-start(bf16[128,64]{0,1:T(8,128)(2,1)S(1)} %get-tuple-element.7), channel_id=1, source_target_pairs={{0,24},{8,0},{16,8},{24,16},{1,25},{9,1},{17,9},{25,17},{2,26},{10... | collective-permute-start | bytes 49160 | tf_op jit(solution)/shard_map/ppermute | solution.py:10
  53.1 4.2 %collective-permute-start.1 = (bf16[1,1,128,384]{3,2,1,0:T(8,128)(2,1)S(1)}, bf16[1,1,128,384]{3,2,1,0:T(8,128)(2,1)S(1)}, u32[]{:S(2)}, u32[]{:S(2)}) collective-permute-start(bf16[1,1,128,384]{3,2,1,0:T(8,128)(2,1)S(1)} %collective-permute-done), channel_id=1, source_target_pairs={{0,7},{1,0},{2,1},{3,2},{4,3},{5,4},{6,5},{7,6},{8,15},{9,8},{10,9... | collective-permute-start | bytes 294920 | tf_op jit(solution)/shard_map/ppermute | solution.py:10
  57.4 32.2 %collective-permute-start.2 = (bf16[1,1,128,384]{3,2,1,0:T(8,128)(2,1)S(1)}, bf16[1,1,128,384]{3,2,1,0:T(8,128)(2,1)S(1)}, u32[]{:S(2)}, u32[]{:S(2)}) collective-permute-start(bf16[1,1,128,384]{3,2,1,0:T(8,128)(2,1)S(1)} %collective-permute-done.1), channel_id=1, source_target_pairs={{0,8},{8,16},{16,24},{24,0},{1,9},{9,17},{17,25},{25,1},{2,10},{10... | collective-permute-start | bytes 294920 | tf_op jit(solution)/shard_map/ppermute | solution.py:20
  84.8 8.2 %collective-permute-start.3 = (bf16[1,1,128,384]{3,2,1,0:T(8,128)(2,1)S(1)}, bf16[1,1,128,384]{3,2,1,0:T(8,128)(2,1)S(1)}, u32[]{:S(2)}, u32[]{:S(2)}) collective-permute-start(bf16[1,1,128,384]{3,2,1,0:T(8,128)(2,1)S(1)} %collective-permute-done.1), channel_id=1, source_target_pairs={{8,0},{16,8},{24,16},{0,24},{9,1},{17,9},{25,17},{1,25},{10,2},{18... | collective-permute-start | bytes 294920 | tf_op jit(solution)/shard_map/ppermute | solution.py:22
  93.0 14.4 %collective-permute-start.5 = (bf16[3,1,128,384]{3,2,1,0:T(8,128)(2,1)S(1)}, bf16[3,1,128,384]{3,2,1,0:T(8,128)(2,1)S(1)}, u32[]{:S(2)}, u32[]{:S(2)}) collective-permute-start(bf16[3,1,128,384]{3,2,1,0:T(8,128)(2,1)S(1)} %constant_dynamic-update-slice_fusion), channel_id=1, source_target_pairs={{1,0},{2,1},{3,2},{4,3},{5,4},{6,5},{7,6},{0,7},{9,8},{10,9},{11,1... | collective-permute-start | bytes 884744 | tf_op jit(solution)/shard_map/ppermute | solution.py:22
  95.5 11.9 %collective-permute-start.4 = (bf16[3,1,128,384]{3,2,1,0:T(8,128)(2,1)S(1)}, bf16[3,1,128,384]{3,2,1,0:T(8,128)(2,1)S(1)}, u32[]{:S(2)}, u32[]{:S(2)}) collective-permute-start(bf16[3,1,128,384]{3,2,1,0:T(8,128)(2,1)S(1)} %constant_dynamic-update-slice_fusion), channel_id=1, source_target_pairs={{0,1},{1,2},{2,3},{3,4},{4,5},{5,6},{6,7},{7,0},{8,9},{9,10},{10,1... | collective-permute-start | bytes 884744 | tf_op jit(solution)/shard_map/ppermute | solution.py:20
  109.2 1.9 %copy-start.1 = (f32[128,64]{1,0:T(8,128)S(1)}, f32[128,64]{1,0:T(8,128)}, u32[]{:S(2)}) copy-start(f32[128,64]{1,0:T(8,128)} %convolution_add_fusion.1) | copy-start | bytes 98308
  109.2 1.9 %copy-start.2 = (bf16[1,1,64,384]{3,2,1,0:T(8,128)(2,1)S(1)}, bf16[1,1,64,384]{3,2,1,0:T(8,128)(2,1)}, u32[]{:S(2)}) copy-start(bf16[1,1,64,384]{3,2,1,0:T(8,128)(2,1)} %param.21) | copy-start | bytes 147460
where the time goes:
time: 112 us
  blocking collectives  68.1 us (61%)
  waiting for transfers between devices  17.4 us (16%)
  starting transfers between devices  12.5 us (11%)
  matrix products  8.11 us (7%)
  other arithmetic  2.8 us (2%)
  local copies, waits for them, and re-layouts  2.28 us (2%)
    psum x1, blocking collectives, per_device(): lax.psum(upward.astype(jnp.bfloat16), 'col').astype(jnp.float32)  30.1 us
    all_gather x1, blocking collectives, per_device(): lax.all_gather(three_rows[:, None].astype(jnp.bfloat16), 'col', axis=1, t...  25.3 us
    ppermute x2, waiting for transfers between devices, padded_2(): lax.ppermute(head, axis, [((i + 1) % count, i) for i in range(count)])  13.2 us
    all_gather x1, blocking collectives, per_device(): lax.all_gather(own_region[None].astype(jnp.bfloat16), 'row', axis=0, tile...  12.6 us
    ppermute x2, starting transfers between devices, padded_2(): lax.ppermute(head, axis, [((i + 1) % count, i) for i in range(count)])  7.24 us
    ppermute x4, waiting for transfers between devices, from_behind(): return lax.ppermute(value, axis, pairs)  4.15 us
    ppermute x4, starting transfers between devices, from_behind(): return lax.ppermute(value, axis, pairs)  3.15 us
  transfers between devices with their start and end apart: 8, of which 3 were waited for; matrix products, arithmetic and copies ran while one was open for 8% of the time, Pallas kernels for 0%

commit v1 on v0

--- a/solution.py
+++ b/solution.py
@@ -71,7 +71,9 @@
     )
     upward = jnp.dot(incoming_leaf, transfer_col[0, 0].astype(jnp.float32), precision=upper_limit)
     row_count = lax.axis_size("row")
-    own_region = lax.psum(upward.astype(jnp.bfloat16), "col").astype(jnp.float32)
+    own_region = jnp.sum(
+        jax.lax.all_gather(upward.astype(jnp.bfloat16), axis_name="col"), axis=0
+    ).astype(jnp.float32)
     regions = lax.all_gather(
         own_region[None].astype(jnp.bfloat16), "row", axis=0, tiled=True
     ).astype(jnp.float32)

time: 112 us -> 103 us (0.920)
  blocking collectives: 68.1 us -> 57.8 us
  starting transfers between devices: 12.5 us -> 16.6 us
  waiting for transfers between devices: 17.4 us -> 15.3 us
    psum x1 -> x0, blocking collectives: 30.1 us -> none  [per_device(): lax.psum(upward.astype(jnp.bfloat16), 'col').astype(jnp.float32)]
    all_gather x0 -> x1, blocking collectives: none -> 22 us  [per_device(): jax.lax.all_gather(upward.astype(jnp.bfloat16), axis_name='col')]
    ppermute x2, waiting for transfers between devices: 0.01 us -> 4.88 us  [padded_2(): lax.ppermute(tail, axis, [(i, (i + 1) % count) for i in range(count)])]
    ppermute x2, waiting for transfers between devices: 13.2 us -> 8.46 us  [padded_2(): lax.ppermute(head, axis, [((i + 1) % count, i) for i in range(count)])]
    all_gather x1, blocking collectives: 12.6 us -> 9.78 us  [per_device(): lax.all_gather(own_region[None].astype(jnp.bfloat16), 'row', axis=0, tile...]
    ppermute x4, starting transfers between devices: 3.15 us -> 5.56 us  [from_behind(): return lax.ppermute(value, axis, pairs)]
    ppermute x4, waiting for transfers between devices: 4.15 us -> 1.98 us  [from_behind(): return lax.ppermute(value, axis, pairs)]
    ppermute x2, starting transfers between devices: 7.24 us -> 8.77 us  [padded_2(): lax.ppermute(head, axis, [((i + 1) % count, i) for i in range(count)])]
  transfers between devices with their start and end apart: 8 -> 8, of which waited for: 3 -> 4; matrix products, arithmetic and copies ran while one was open for 8% -> 7% of each run, Pallas kernels for 0% -> 0%
where the time goes in v1:
time: 103 us
  blocking collectives  57.8 us (56%)
  starting transfers between devices  16.6 us (16%)
  waiting for transfers between devices  15.3 us (15%)
  matrix products  7.13 us (7%)
  other arithmetic  2.89 us (3%)
  local copies, waits for them, and re-layouts  2.3 us (2%)
    all_gather x1, blocking collectives, per_device(): lax.all_gather(three_rows[:, None].astype(jnp.bfloat16), 'col', axis=1, t...  26 us
    all_gather x1, blocking collectives, per_device(): jax.lax.all_gather(upward.astype(jnp.bfloat16), axis_name='col')  22 us
    all_gather x1, blocking collectives, per_device(): lax.all_gather(own_region[None].astype(jnp.bfloat16), 'row', axis=0, tile...  9.78 us
    ppermute x2, starting transfers between devices, padded_2(): lax.ppermute(head, axis, [((i + 1) % count, i) for i in range(count)])  8.77 us
    ppermute x2, waiting for transfers between devices, padded_2(): lax.ppermute(head, axis, [((i + 1) % count, i) for i in range(count)])  8.46 us
    ppermute x4, starting transfers between devices, from_behind(): return lax.ppermute(value, axis, pairs)  5.56 us
    ppermute x2, waiting for transfers between devices, padded_2(): lax.ppermute(tail, axis, [(i, (i + 1) % count) for i in range(count)])  4.88 us
    ppermute x2, starting transfers between devices, padded_2(): lax.ppermute(tail, axis, [(i, (i + 1) % count) for i in range(count)])  2.25 us
  transfers between devices with their start and end apart: 8, of which 4 were waited for; matrix products, arithmetic and copies ran while one was open for 7% of the time, Pallas kernels for 0%

profile of v1, /device:TPU:1, one launch (start us, length us, event | category | flops | bytes accessed | tf_op | source)
XLA Modules:
  0.0 102.8 jit_solution(4839369964947182886)
XLA Ops:
  0.0 0.0 copy-start
  0.0 0.0 copy-start.4
  0.0 0.0 copy-start.3
  0.0 0.1 collective-permute-start
  0.1 1.2 %fusion.36 = (bf16[128,64]{0,1:T(8,128)(2,1)S(1)}, f32[128,64]{0,1:T(8,128)S(1)}) fusion(bf16[1,1,64,384]{3,2,1,0:T(8,128)(2,1)} %param.15, bf16[1,1,128,384]{3,2,1,0:T(8,128)(2,1)} %param.11), kind=kOutput, calls=%fused_computation.64 | convolution fusion | flops 6299648 | bytes 196608 | tf_op jit(solution)/shard_map/dot_general | solution.py:54
  1.3 2.7 %collective-permute-start.7 = (bf16[128,64]{0,1:T(8,128)(2,1)S(1)}, bf16[128,64]{0,1:T(8,128)(2,1)S(1)}, u32[]{:S(2)}, u32[]{:S(2)}) collective-permute-start(bf16[128,64]{0,1:T(8,128)(2,1)S(1)} %get-tuple-element.7), channel_id=1, source_target_pairs={{0,16},{8,24},{16,0},{24,8},{1,17},{9,25},{17,1},{25,9},{2,18},{10... | collective-permute-start | bytes 49160 | tf_op jit(solution)/shard_map/ppermute | solution.py:10
  4.0 0.4 collective-permute-start.6
  4.4 0.7 fusion.29
  5.7 0.7 compare_and_fusion.1
  6.3 0.9 convolution_convert_fusion
  7.3 22.0 %all-gather = bf16[1024,64]{0,1:T(8,128)(2,1)S(1)} all-gather(bf16[128,64]{0,1:T(8,128)(2,1)S(1)} %convolution_convert_fusion), channel_id=2, replica_groups=mesh['row'=4,'col'=8] {'col'}, dimensions={0}, use_global_device_ids=true | all-gather | bytes 147456 | tf_op jit(solution)/shard_map/all_gather | solution.py:75
  29.3 0.1 bitcast_reduce_fusion
  29.4 9.8 %all-gather.1 = bf16[512,64]{0,1:T(8,128)(2,1)S(1)} all-gather(bf16[128,64]{0,1:T(8,128)(2,1)S(1)} %bitcast_reduce_fusion), channel_id=3, replica_groups=mesh['row'=4,'col'=8] {'row'}, dimensions={0}, use_global_device_ids=true | all-gather | bytes 81920 | tf_op jit(solution)/shard_map/all_gather | solution.py:77
  39.2 0.7 fusion.30
  39.9 0.7 compare_and_fusion
  40.6 0.6 gather_fusion.1
  41.1 1.1 %convolution_bitcast_fusion = f32[128,64]{0,1:T(8,128)S(1)} fusion(f32[4,128,64]{1,2,0:T(8,128)S(1)} %gather_fusion.1, bf16[1,4,64,64]{3,2,1,0:T(8,128)(2,1)} %param.18, f32[4]{0:T(128)S(1)} %get-tuple-element.6, pred[4]{0:T(512)(128)(4,1)S(1)} %get-tuple-element.5), kind=kOutput, calls=%fused_computation.9 | convolution fusion | flops 25231360 | bytes 196628 | tf_op jit(solution)/shard_map/fvk,fkl->vl/dot_general | solution.py:83
  42.3 0.0 collective-permute-done
  42.3 2.4 %collective-permute-start.1 = (bf16[1,1,128,384]{3,2,1,0:T(8,128)(2,1)S(1)}, bf16[1,1,128,384]{3,2,1,0:T(8,128)(2,1)S(1)}, u32[]{:S(2)}, u32[]{:S(2)}) collective-permute-start(bf16[1,1,128,384]{3,2,1,0:T(8,128)(2,1)S(1)} %collective-permute-done), channel_id=1, source_target_pairs={{0,7},{1,0},{2,1},{3,2},{4,3},{5,4},{6,5},{7,6},{8,15},{9,8},{10,9... | collective-permute-start | bytes 294920 | tf_op jit(solution)/shard_map/ppermute | solution.py:10
  44.7 0.0 collective-permute-done.7
  44.7 0.0 collective-permute-done.6
  44.7 2.0 %collective-permute-done.1 = bf16[1,1,128,384]{3,2,1,0:T(8,128)(2,1)S(1)} collective-permute-done((bf16[1,1,128,384]{3,2,1,0:T(8,128)(2,1)S(1)}, bf16[1,1,128,384]{3,2,1,0:T(8,128)(2,1)S(1)}, u32[]{:S(2)}, u32[]{:S(2)}) %collective-permute-start.1) | collective-permute-done | bytes 98336 | tf_op jit(solution)/shard_map/ppermute | solution.py:10
  46.7 2.2 %collective-permute-start.2 = (bf16[1,1,128,384]{3,2,1,0:T(8,128)(2,1)S(1)}, bf16[1,1,128,384]{3,2,1,0:T(8,128)(2,1)S(1)}, u32[]{:S(2)}, u32[]{:S(2)}) collective-permute-start(bf16[1,1,128,384]{3,2,1,0:T(8,128)(2,1)S(1)} %collective-permute-done.1), channel_id=1, source_target_pairs={{0,8},{8,16},{16,24},{24,0},{1,9},{9,17},{17,25},{25,1},{2,10},{10... | collective-permute-start | bytes 294920 | tf_op jit(solution)/shard_map/ppermute | solution.py:20
  48.9 26.0 %all_gather.12 = bf16[3,8,128,64]{2,3,1,0:T(8,128)(2,1)S(1)} all-gather(bf16[3,1,128,64]{2,3,1,0:T(8,128)(2,1)S(1)} %pad_maximum_fusion.1), channel_id=1, replica_groups=mesh['row'=4,'col'=8] {'col'}, dimensions={1}, use_global_device_ids=true | all-gather | bytes 442368 | tf_op jit(solution)/shard_map/all_gather | solution.py:64
  74.9 4.3 %collective-permute-start.3 = (bf16[1,1,128,384]{3,2,1,0:T(8,128)(2,1)S(1)}, bf16[1,1,128,384]{3,2,1,0:T(8,128)(2,1)S(1)}, u32[]{:S(2)}, u32[]{:S(2)}) collective-permute-start(bf16[1,1,128,384]{3,2,1,0:T(8,128)(2,1)S(1)} %collective-permute-done.1), channel_id=1, source_target_pairs={{8,0},{16,8},{24,16},{0,24},{9,1},{17,9},{25,17},{1,25},{10,2},{18... | collective-permute-start | bytes 294920 | tf_op jit(solution)/shard_map/ppermute | solution.py:22
  79.2 0.0 collective-permute-done.2
  79.3 3.5 %collective-permute-done.3 = bf16[1,1,128,384]{3,2,1,0:T(8,128)(2,1)S(1)} collective-permute-done((bf16[1,1,128,384]{3,2,1,0:T(8,128)(2,1)S(1)}, bf16[1,1,128,384]{3,2,1,0:T(8,128)(2,1)S(1)}, u32[]{:S(2)}, u32[]{:S(2)}) %collective-permute-start.3) | collective-permute-done | bytes 98336 | tf_op jit(solution)/shard_map/ppermute | solution.py:22
  82.8 4.5 %collective-permute-start.5 = (bf16[3,1,128,384]{3,2,1,0:T(8,128)(2,1)S(1)}, bf16[3,1,128,384]{3,2,1,0:T(8,128)(2,1)S(1)}, u32[]{:S(2)}, u32[]{:S(2)}) collective-permute-start(bf16[3,1,128,384]{3,2,1,0:T(8,128)(2,1)S(1)} %constant_dynamic-update-slice_fusion), channel_id=1, source_target_pairs={{1,0},{2,1},{3,2},{4,3},{5,4},{6,5},{7,6},{0,7},{9,8},{10,9},{11,1... | collective-permute-start | bytes 884744 | tf_op jit(solution)/shard_map/ppermute | solution.py:22
  87.3 0.0 collective-permute-start.4
  87.3 0.0 copy-done.4
  87.3 0.3 convolution_bitcast_fusion.1
  87.5 0.0 copy-done.3
  87.6 0.8 convolution_add_fusion.1
  88.4 4.9 %collective-permute-done.5 = bf16[3,1,128,384]{3,2,1,0:T(8,128)(2,1)S(1)} collective-permute-done((bf16[3,1,128,384]{3,2,1,0:T(8,128)(2,1)S(1)}, bf16[3,1,128,384]{3,2,1,0:T(8,128)(2,1)S(1)}, u32[]{:S(2)}, u32[]{:S(2)}) %collective-permute-start.5) | collective-permute-done | bytes 294944 | tf_op jit(solution)/shard_map/ppermute | solution.py:22
  93.3 4.9 %collective-permute-done.4 = bf16[3,1,128,384]{3,2,1,0:T(8,128)(2,1)S(1)} collective-permute-done((bf16[3,1,128,384]{3,2,1,0:T(8,128)(2,1)S(1)}, bf16[3,1,128,384]{3,2,1,0:T(8,128)(2,1)S(1)}, u32[]{:S(2)}, u32[]{:S(2)}) %collective-permute-start.4) | collective-permute-done | bytes 294944 | tf_op jit(solution)/shard_map/ppermute | solution.py:20
  98.2 0.1 pad_maximum_fusion
  98.3 1.7 %gather_fusion = bf16[9,128,384]{2,1,0:T(8,128)(2,1)} fusion(bf16[9,128,384]{2,1,0:T(8,128)(2,1)S(1)} %bitcast.74, s32[1024]{0:T(1024)S(1)} %pad_clamp_fusion.1), kind=kCustom, calls=%fused_computation | custom fusion | bytes 1769508 | tf_op jit(solution)/shard_map/jit(_take)/gather | solution.py:47
  100.0 0.0 copy-start.1
  100.0 0.0 copy-start.2
  100.0 0.0 copy-done
  100.0 1.9 %fusion.2 = f32[128,384]{1,0:T(8,128)S(1)} fusion(bf16[1,1,9,384,384]{4,3,2,1,0:T(8,128)(2,1)S(1)} %copy-done, bf16[9,128,384]{2,1,0:T(8,128)(2,1)} %gather_fusion, pred[9]{0:T(512)(128)(4,1)S(1)} %get-tuple-element.9, pred[9]{0:T(512)(128)(4,1)S(1)} %get-tuple-element.10), kind=kOutput, calls=%fused_computation.5 | convolution fusion | flops 340623360 | bytes 3735570 | tf_op jit(solution)/shard_map/svp,spq->vq/dot_general | solution.py:51
  101.8 0.0 copy-done.1
  101.9 0.0 copy-done.2
  101.9 0.9 fusion.6
  (8 shorter events, 0.1 us)
Async XLA Ops:
  0.0 100.0 %copy-start = (bf16[1,1,9,384,384]{4,3,2,1,0:T(8,128)(2,1)S(1)}, bf16[1,1,9,384,384]{4,3,2,1,0:T(8,128)(2,1)}, u32[]{:S(2)}) copy-start(bf16[1,1,9,384,384]{4,3,2,1,0:T(8,128)(2,1)} %param.12) | copy-start | bytes 7962628
  0.0 87.3 %copy-start.4 = (bf16[1,1,3,5,64,64]{5,4,3,2,1,0:T(8,128)(2,1)S(1)}, bf16[1,1,3,5,64,64]{5,4,3,2,1,0:T(8,128)(2,1)}, u32[]{:S(2)}) copy-start(bf16[1,1,3,5,64,64]{5,4,3,2,1,0:T(8,128)(2,1)} %param.17) | copy-start | bytes 368644
  0.0 87.5 %copy-start.3 = (bf16[1,1,64,64]{3,2,1,0:T(8,128)(2,1)S(1)}, bf16[1,1,64,64]{3,2,1,0:T(8,128)(2,1)}, u32[]{:S(2)}) copy-start(bf16[1,1,64,64]{3,2,1,0:T(8,128)(2,1)} %param.20) | copy-start | bytes 24580
  0.0 42.3 %collective-permute-start = (bf16[1,1,128,384]{3,2,1,0:T(8,128)(2,1)}, bf16[1,1,128,384]{3,2,1,0:T(8,128)(2,1)S(1)}, u32[]{:S(2)}, u32[]{:S(2)}) collective-permute-start(bf16[1,1,128,384]{3,2,1,0:T(8,128)(2,1)} %param.11), channel_id=1, source_target_pairs={{0,24},{8,0},{16,8},{24,16},{1,25},{9,1},{17,9},{25,17},{2,26},{10... | collective-permute-start | bytes 294920 | tf_op jit(solution)/shard_map/ppermute | solution.py:10
  1.3 43.4 %collective-permute-start.7 = (bf16[128,64]{0,1:T(8,128)(2,1)S(1)}, bf16[128,64]{0,1:T(8,128)(2,1)S(1)}, u32[]{:S(2)}, u32[]{:S(2)}) collective-permute-start(bf16[128,64]{0,1:T(8,128)(2,1)S(1)} %get-tuple-element.7), channel_id=1, source_target_pairs={{0,16},{8,24},{16,0},{24,8},{1,17},{9,25},{17,1},{25,9},{2,18},{10... | collective-permute-start | bytes 49160 | tf_op jit(solution)/shard_map/ppermute | solution.py:10
  4.0 40.7 %collective-permute-start.6 = (bf16[128,64]{0,1:T(8,128)(2,1)S(1)}, bf16[128,64]{0,1:T(8,128)(2,1)S(1)}, u32[]{:S(2)}, u32[]{:S(2)}) collective-permute-start(bf16[128,64]{0,1:T(8,128)(2,1)S(1)} %get-tuple-element.7), channel_id=1, source_target_pairs={{0,24},{8,0},{16,8},{24,16},{1,25},{9,1},{17,9},{25,17},{2,26},{10... | collective-permute-start | bytes 49160 | tf_op jit(solution)/shard_map/ppermute | solution.py:10
  42.3 4.4 %collective-permute-start.1 = (bf16[1,1,128,384]{3,2,1,0:T(8,128)(2,1)S(1)}, bf16[1,1,128,384]{3,2,1,0:T(8,128)(2,1)S(1)}, u32[]{:S(2)}, u32[]{:S(2)}) collective-permute-start(bf16[1,1,128,384]{3,2,1,0:T(8,128)(2,1)S(1)} %collective-permute-done), channel_id=1, source_target_pairs={{0,7},{1,0},{2,1},{3,2},{4,3},{5,4},{6,5},{7,6},{8,15},{9,8},{10,9... | collective-permute-start | bytes 294920 | tf_op jit(solution)/shard_map/ppermute | solution.py:10
  46.7 32.5 %collective-permute-start.2 = (bf16[1,1,128,384]{3,2,1,0:T(8,128)(2,1)S(1)}, bf16[1,1,128,384]{3,2,1,0:T(8,128)(2,1)S(1)}, u32[]{:S(2)}, u32[]{:S(2)}) collective-permute-start(bf16[1,1,128,384]{3,2,1,0:T(8,128)(2,1)S(1)} %collective-permute-done.1), channel_id=1, source_target_pairs={{0,8},{8,16},{16,24},{24,0},{1,9},{9,17},{17,25},{25,1},{2,10},{10... | collective-permute-start | bytes 294920 | tf_op jit(solution)/shard_map/ppermute | solution.py:20
  74.9 7.9 %collective-permute-start.3 = (bf16[1,1,128,384]{3,2,1,0:T(8,128)(2,1)S(1)}, bf16[1,1,128,384]{3,2,1,0:T(8,128)(2,1)S(1)}, u32[]{:S(2)}, u32[]{:S(2)}) collective-permute-start(bf16[1,1,128,384]{3,2,1,0:T(8,128)(2,1)S(1)} %collective-permute-done.1), channel_id=1, source_target_pairs={{8,0},{16,8},{24,16},{0,24},{9,1},{17,9},{25,17},{1,25},{10,2},{18... | collective-permute-start | bytes 294920 | tf_op jit(solution)/shard_map/ppermute | solution.py:22
  82.8 10.5 %collective-permute-start.5 = (bf16[3,1,128,384]{3,2,1,0:T(8,128)(2,1)S(1)}, bf16[3,1,128,384]{3,2,1,0:T(8,128)(2,1)S(1)}, u32[]{:S(2)}, u32[]{:S(2)}) collective-permute-start(bf16[3,1,128,384]{3,2,1,0:T(8,128)(2,1)S(1)} %constant_dynamic-update-slice_fusion), channel_id=1, source_target_pairs={{1,0},{2,1},{3,2},{4,3},{5,4},{6,5},{7,6},{0,7},{9,8},{10,9},{11,1... | collective-permute-start | bytes 884744 | tf_op jit(solution)/shard_map/ppermute | solution.py:22
  87.3 10.9 %collective-permute-start.4 = (bf16[3,1,128,384]{3,2,1,0:T(8,128)(2,1)S(1)}, bf16[3,1,128,384]{3,2,1,0:T(8,128)(2,1)S(1)}, u32[]{:S(2)}, u32[]{:S(2)}) collective-permute-start(bf16[3,1,128,384]{3,2,1,0:T(8,128)(2,1)S(1)} %constant_dynamic-update-slice_fusion), channel_id=1, source_target_pairs={{0,1},{1,2},{2,3},{3,4},{4,5},{5,6},{6,7},{7,0},{8,9},{9,10},{10,1... | collective-permute-start | bytes 884744 | tf_op jit(solution)/shard_map/ppermute | solution.py:20
  100.0 1.9 %copy-start.1 = (f32[128,64]{0,1:T(8,128)S(1)}, f32[128,64]{0,1:T(8,128)}, u32[]{:S(2)}) copy-start(f32[128,64]{0,1:T(8,128)} %convolution_add_fusion.1) | copy-start | bytes 98308
  100.0 1.9 %copy-start.2 = (bf16[1,1,64,384]{3,2,1,0:T(8,128)(2,1)S(1)}, bf16[1,1,64,384]{3,2,1,0:T(8,128)(2,1)}, u32[]{:S(2)}) copy-start(bf16[1,1,64,384]{3,2,1,0:T(8,128)(2,1)} %param.21) | copy-start | bytes 147460
